TPU v7x, 128 devices: a whole 4x4x4 slice. The times are simulated.
128 devices in a mesh: data: 1, branch: 128 (over z, y, x, core).
Axes of the slice: x: 4, y: 4, z: 4, core: 2. Of those that a mesh axis runs over, the one named last changes fastest.
Arguments:
- x: bfloat16 [1, 1024, 3072], P('data', 'branch')
- h: bfloat16 [1, 1024, 3072], P('data', 'branch')
- in_qkv: bfloat16 [2, 1, 3072, 9216], replicated
- in_proj: bfloat16 [2, 1, 24, 128, 3072], replicated
- in_up: bfloat16 [2, 1, 3072, 12288], replicated
- in_down: bfloat16 [2, 1, 12288, 3072], replicated
- tail_qkv: bfloat16 [1, 3072, 9216], replicated
- tail_proj: bfloat16 [1, 24, 128, 3072], replicated
- tail_up: bfloat16 [1, 3072, 12288], replicated
- tail_down: bfloat16 [1, 12288, 3072], replicated
- z_hint: bfloat16 [3072, 3072], replicated
- z_out: bfloat16 [1, 3072, 3072], replicated
- w_final: bfloat16 [3072, 3072], replicated
Outputs:
- output: bfloat16 [1, 1024, 3072], P('data', 'branch')
All inputs are finite; a program needn't handle non-finite values.
Results may differ from a plain program's by a relative error of at most 0.019224.
Values are sent between devices in bfloat16 or wider.
A program may use at most 1.5 GiB of HBM per device.

v0:
```python
import jax
import jax.numpy as jnp
from jax import lax
from jax.sharding import PartitionSpec as P

LN_EPS = 1e-6


def layer_norm(residual):
    residual_f32 = residual.astype(jnp.float32)
    centred = residual_f32 - jnp.mean(residual_f32, axis=-1, keepdims=True)
    variance = jnp.mean(centred * centred, axis=-1, keepdims=True)
    return (centred * lax.rsqrt(variance + LN_EPS)).astype(jnp.bfloat16)


def transformer_block(residual, w_qkv, w_proj, w_up, w_down, gather_kv):
    num_rows = residual.shape[0]
    num_heads, head_dim = w_proj.shape[0], w_proj.shape[1]
    qkv_rows = jnp.dot(layer_norm(residual), w_qkv, preferred_element_type=jnp.float32).astype(jnp.bfloat16)
    qkv_rows = qkv_rows.reshape(num_rows, 3, num_heads, head_dim)
    kv_rows = gather_kv(qkv_rows[:, 1:])
    scores = jnp.einsum('qhe,khe->hqk', qkv_rows[:, 0], kv_rows[:, 0], preferred_element_type=jnp.float32) * head_dim ** -0.5
    attn_probs = jax.nn.softmax(scores, axis=-1).astype(jnp.bfloat16)
    attn_out = jnp.einsum('hqk,khe->qhe', attn_probs, kv_rows[:, 1], preferred_element_type=jnp.float32).astype(jnp.bfloat16)
    proj_out = jnp.einsum('qhe,hed->qd', attn_out, w_proj, preferred_element_type=jnp.float32).astype(jnp.bfloat16)
    residual = (residual.astype(jnp.float32) + proj_out.astype(jnp.float32)).astype(jnp.bfloat16)
    hidden = jax.nn.gelu(jnp.dot(layer_norm(residual), w_up, preferred_element_type=jnp.float32), approximate=True).astype(jnp.bfloat16)
    mlp_out = jnp.dot(hidden, w_down, preferred_element_type=jnp.float32).astype(jnp.bfloat16)
    return (residual.astype(jnp.float32) + mlp_out.astype(jnp.float32)).astype(jnp.bfloat16)


def branch_weight(weight_stack, layer_idx, branch_id):
    return lax.dynamic_index_in_dim(weight_stack[:, layer_idx], branch_id, axis=0, keepdims=False)


def solution(mesh):
    group_size = mesh.shape['branch']
    half_size = group_size // 2
    swap_perm = [(dev_idx, (dev_idx + half_size) % group_size) for dev_idx in range(group_size)]
    base_to_ctrl = [(dev_idx, dev_idx + half_size) for dev_idx in range(half_size)]
    ctrl_to_base = [(dev_idx + half_size, dev_idx) for dev_idx in range(half_size)]
    dist_list = [2 ** exponent for exponent in range(16) if 2 ** exponent < half_size]
    gather_perms = [[(dev_idx, dev_idx ^ step_dist) for dev_idx in range(group_size)] for step_dist in dist_list]

    def gather_kv(kv_local):
        gathered = kv_local
        for perm_list in gather_perms:
            gathered = jnp.concatenate([gathered, lax.ppermute(gathered, 'branch', perm_list)], axis=0)
        return gathered

    def device_step(x_blk, hint_blk, in_qkv, in_proj, in_up, in_down, tail_qkv, tail_proj, tail_up, tail_down, z_hint, z_out, w_final):
        dev_index = lax.axis_index('branch')
        is_base = dev_index < half_size
        branch_id = dev_index // half_size
        own_x = x_blk[0]
        own_rows = own_x.shape[0]
        partner_x = lax.ppermute(own_x, 'branch', swap_perm)
        hint_proj = jnp.dot(hint_blk[0], z_hint, preferred_element_type=jnp.float32).astype(jnp.bfloat16)
        partner_hint = lax.ppermute(hint_proj, 'branch', base_to_ctrl)
        pair_x = jnp.concatenate([jnp.where(is_base, own_x, partner_x), jnp.where(is_base, partner_x, own_x)], axis=0)
        pair_hint = jnp.concatenate([partner_hint, hint_proj], axis=0)
        hint_gate = jnp.where(is_base, 0.0, 1.0)
        act_state = (pair_x.astype(jnp.float32) + hint_gate * pair_hint.astype(jnp.float32)).astype(jnp.bfloat16)
        for layer_idx in range(in_qkv.shape[1]):
            block_out = transformer_block(act_state, branch_weight(in_qkv, layer_idx, branch_id), branch_weight(in_proj, layer_idx, branch_id), branch_weight(in_up, layer_idx, branch_id), branch_weight(in_down, layer_idx, branch_id), gather_kv)
            ctrl_resid = jnp.dot(block_out, z_out[layer_idx], preferred_element_type=jnp.float32).astype(jnp.bfloat16)
            arrived = lax.ppermute(ctrl_resid, 'branch', ctrl_to_base)
            act_state = (block_out.astype(jnp.float32) + arrived.astype(jnp.float32)).astype(jnp.bfloat16)
        for layer_idx in range(tail_qkv.shape[0]):
            act_state = transformer_block(act_state, tail_qkv[layer_idx], tail_proj[layer_idx], tail_up[layer_idx], tail_down[layer_idx], gather_kv)
        y_pair = jnp.dot(layer_norm(act_state), w_final, preferred_element_type=jnp.float32).astype(jnp.bfloat16)
        y_high = lax.ppermute(y_pair[own_rows:], 'branch', base_to_ctrl)
        return jnp.where(is_base, y_pair[:own_rows], y_high)[None]

    act_spec = P('data', 'branch', None)
    return jax.shard_map(device_step, mesh=mesh, in_specs=(act_spec, act_spec) + (P(),) * 11, out_specs=act_spec, check_vma=False)
```

profile of v0, /device:TPU:1, one launch (start us, length us, event | category | flops | bytes accessed | tf_op | source)
XLA Modules:
  0.0 778.3 jit_solution(10408966292531357225)
XLA Ops:
  0.0 4.4 collective-permute-start
  4.4 8.9 %convolution_convert_fusion.1 = bf16[8,3072]{1,0:T(8,128)(2,1)S(1)} fusion(bf16[3072,3072]{1,0:T(8,128)(2,1)} %param.23, bf16[1,8,3072]{2,1,0:T(8,128)(2,1)S(1)} %copy-done), kind=kOutput, calls=%fused_computation.57 | convolution fusion | flops 151019520 | bytes 18972672 | tf_op jit(solution)/shard_map/dot_general | solution.py:58
  13.3 2.7 collective-permute-start.1
  16.1 1.1 collective-permute-done.1
  17.4 0.2 fusion.163
  17.6 20.0 %fusion.106 = bf16[2,8,72,128]{3,1,2,0:T(8,128)(2,1)S(1)} fusion(bf16[2,1,3072,9216]{3,2,1,0:T(8,128)(2,1)} %param.15, s32[]{:T(128)S(6)} %select_n.40, bf16[16,3072]{1,0:T(8,128)(2,1)S(1)} %get-tuple-element.8, f32[16]{0:T(128)S(1)} %add_rsqrt_fusion.4, f32[16]{0:T(128)S(1)} %broadcast_multiply_fusion.4), kind=kOutput, calls=%fused_computation.72 | convolution fusion | flops 906313728 | bytes 57016452 | tf_op jit(solution)/shard_map/dot_general | solution.py:19
  37.7 0.8 constant_dynamic-update-slice_fusion.10
  38.5 1.5 collective-permute-start.2
  40.0 1.1 collective-permute-done.2
  41.1 1.3 collective-permute-start.3
  42.4 9.1 %collective-permute-done.3 = bf16[32,2,24,128]{3,0,2,1:T(8,128)(2,1)S(1)} collective-permute-done((bf16[32,2,24,128]{3,0,2,1:T(8,128)(2,1)S(1)}, bf16[32,2,24,128]{3,0,2,1:T(8,128)(2,1)S(1)}, u32[]{:S(2)}, u32[]{:S(2)}) %collective-permute-start.3) | collective-permute-done | bytes 393248 | tf_op jit(solution)/shard_map/ppermute | solution.py:48
  51.6 2.8 collective-permute-start.4
  54.4 16.6 %collective-permute-done.4 = bf16[64,2,24,128]{3,0,2,1:T(8,128)(2,1)S(1)} collective-permute-done((bf16[64,2,24,128]{3,0,2,1:T(8,128)(2,1)S(1)}, bf16[64,2,24,128]{3,0,2,1:T(8,128)(2,1)S(1)}, u32[]{:S(2)}, u32[]{:S(2)}) %collective-permute-start.4) | collective-permute-done | bytes 786464 | tf_op jit(solution)/shard_map/ppermute | solution.py:48
  71.2 1.4 collective-permute-start.5
  72.6 0.8 constant_dynamic-update-slice_fusion.9
  73.4 1.0 constant_dynamic-update-slice_fusion.8
  74.4 1.6 constant_dynamic-update-slice_fusion.7
  76.1 28.9 %collective-permute-done.5 = bf16[128,2,24,128]{3,0,2,1:T(8,128)(2,1)S(1)} collective-permute-done((bf16[128,2,24,128]{3,0,2,1:T(8,128)(2,1)S(1)}, bf16[128,2,24,128]{3,0,2,1:T(8,128)(2,1)S(1)}, u32[]{:S(2)}, u32[]{:S(2)}) %collective-permute-start.5) | collective-permute-done | bytes 1572896 | tf_op jit(solution)/shard_map/ppermute | solution.py:48
  104.9 2.6 constant_dynamic-update-slice_fusion.6
  107.5 2.9 collective-permute-start.6
  110.4 65.1 %collective-permute-done.6 = bf16[256,2,24,128]{3,0,2,1:T(8,128)(2,1)S(1)} collective-permute-done((bf16[256,2,24,128]{3,0,2,1:T(8,128)(2,1)S(1)}, bf16[256,2,24,128]{3,0,2,1:T(8,128)(2,1)S(1)}, u32[]{:S(2)}, u32[]{:S(2)}) %collective-permute-start.6) | collective-permute-done | bytes 3145760 | tf_op jit(solution)/shard_map/ppermute | solution.py:48
  175.5 3.7 constant_dynamic-update-slice_fusion.5
  179.2 0.9 collective-permute-start.7
  180.1 132.0 %collective-permute-done.7 = bf16[512,2,24,128]{3,0,2,1:T(8,128)(2,1)S(1)} collective-permute-done((bf16[512,2,24,128]{3,0,2,1:T(8,128)(2,1)S(1)}, bf16[512,2,24,128]{3,0,2,1:T(8,128)(2,1)S(1)}, u32[]{:S(2)}, u32[]{:S(2)}) %collective-permute-start.7) | collective-permute-done | bytes 6291488 | tf_op jit(solution)/shard_map/ppermute | solution.py:48
  312.2 3.7 constant_dynamic-update-slice_fusion.11
  315.9 4.7 fusion.208
  320.6 10.2 %fusion.209 = (f32[16]{0:T(128)S(1)}, f32[16,3072]{1,0:T(8,128)S(1)}) fusion(bf16[2,1,24,128,3072]{4,3,2,1,0:T(8,128)(2,1)} %param.16, s32[]{:T(128)S(6)} %select_n.40, bf16[1024,2,24,128]{3,0,2,1:T(8,128)(2,1)} %constant_dynamic-update-slice_fusion.11, f32[24,16,1024]{2,1,0:T(8,128)S(1)} %get-tuple-element.48, f32[24,16]{1,0:T(8,128)S(1)} %get-tuple-element.47, ...), kind=kOutput, calls=%fused_computation.209 | convolution fusion | flops 403832832 | bytes 27035204 | tf_op jit(solution)/shard_map/qhe,hed->qd/dot_general | solution.py:25
  330.8 0.2 multiply_reduce_fusion.4
  331.1 25.6 %fusion.125.clone.5 = bf16[16,12288]{1,0:T(8,128)(2,1)S(1)} fusion(bf16[2,1,3072,12288]{3,2,1,0:T(8,128)(2,1)} %param.17, s32[]{:T(128)S(6)} %select_n.40, f32[16,3072]{1,0:T(8,128)S(1)} %get-tuple-element.50, f32[16]{0:T(128)S(1)} %add_rsqrt_fusion.3, f32[16]{0:T(128)S(1)} %broadcast_multiply_fusion.3), kind=kOutput, calls=%fused_computation.85.clone.clone.clone.2 | convolution fusion | flops 1209876480 | bytes 76087424 | tf_op jit(solution)/shard_map/dot_general | solution.py:27
  356.7 25.3 %fusion.97 = bf16[16,3072]{1,0:T(8,128)(2,1)S(1)} fusion(f32[16,3072]{1,0:T(8,128)S(1)} %get-tuple-element.50, bf16[2,1,12288,3072]{3,2,1,0:T(8,128)(2,1)} %param.18, s32[]{:T(128)S(6)} %select_n.40, bf16[16,12288]{1,0:T(8,128)(2,1)S(1)} %fusion.125.clone.5), kind=kOutput, calls=%fused_computation.56 | convolution fusion | flops 1208156160 | bytes 76185600 | tf_op jit(solution)/shard_map/dot_general | solution.py:28
  382.0 8.9 %fusion.70 = bf16[16,3072]{1,0:T(8,128)(2,1)S(1)} fusion(bf16[16,3072]{1,0:T(8,128)(2,1)S(1)} %fusion.97, bf16[1,3072,3072]{2,1,0:T(8,128)(2,1)} %param.24), kind=kOutput, calls=%fused_computation.46 | convolution fusion | flops 302039040 | bytes 19070976 | tf_op jit(solution)/shard_map/dot_general | solution.py:66
  390.9 1.3 collective-permute-start.8
  392.2 5.6 collective-permute-done.8
  397.9 0.2 fusion.161
  398.1 20.2 %fusion.109 = bf16[2,8,72,128]{3,1,2,0:T(8,128)(2,1)S(1)} fusion(bf16[1,3072,9216]{2,1,0:T(8,128)(2,1)} %param.19, bf16[16,3072]{1,0:T(8,128)(2,1)S(1)} %get-tuple-element.6, f32[16]{0:T(128)S(1)} %add_rsqrt_fusion.2, f32[16]{0:T(128)S(1)} %broadcast_multiply_fusion.2), kind=kOutput, calls=%fused_computation.73 | convolution fusion | flops 906313728 | bytes 57016448 | tf_op jit(solution)/shard_map/dot_general | solution.py:19
  418.6 6.4 collective-permute-start.9
  425.0 1.1 collective-permute-done.9
  426.1 1.3 collective-permute-start.10
  427.4 9.1 %collective-permute-done.10 = bf16[32,2,24,128]{3,0,2,1:T(8,128)(2,1)S(1)} collective-permute-done((bf16[32,2,24,128]{3,0,2,1:T(8,128)(2,1)S(1)}, bf16[32,2,24,128]{3,0,2,1:T(8,128)(2,1)S(1)}, u32[]{:S(2)}, u32[]{:S(2)}) %collective-permute-start.10) | collective-permute-done | bytes 393248 | tf_op jit(solution)/shard_map/ppermute | solution.py:48
  436.6 2.8 collective-permute-start.11
  439.4 16.6 %collective-permute-done.11 = bf16[64,2,24,128]{3,0,2,1:T(8,128)(2,1)S(1)} collective-permute-done((bf16[64,2,24,128]{3,0,2,1:T(8,128)(2,1)S(1)}, bf16[64,2,24,128]{3,0,2,1:T(8,128)(2,1)S(1)}, u32[]{:S(2)}, u32[]{:S(2)}) %collective-permute-start.11) | collective-permute-done | bytes 786464 | tf_op jit(solution)/shard_map/ppermute | solution.py:48
  456.2 1.4 collective-permute-start.12
  457.7 0.3 constant_dynamic-update-slice_fusion.26
  458.0 0.7 constant_dynamic-update-slice_fusion.25
  458.8 31.1 %collective-permute-done.12 = bf16[128,2,24,128]{3,0,2,1:T(8,128)(2,1)S(1)} collective-permute-done((bf16[128,2,24,128]{3,0,2,1:T(8,128)(2,1)S(1)}, bf16[128,2,24,128]{3,0,2,1:T(8,128)(2,1)S(1)}, u32[]{:S(2)}, u32[]{:S(2)}) %collective-permute-start.12) | collective-permute-done | bytes 1572896 | tf_op jit(solution)/shard_map/ppermute | solution.py:48
  489.9 1.5 constant_dynamic-update-slice_fusion.24
  491.4 3.0 collective-permute-start.13
  494.4 65.1 %collective-permute-done.13 = bf16[256,2,24,128]{3,0,2,1:T(8,128)(2,1)S(1)} collective-permute-done((bf16[256,2,24,128]{3,0,2,1:T(8,128)(2,1)S(1)}, bf16[256,2,24,128]{3,0,2,1:T(8,128)(2,1)S(1)}, u32[]{:S(2)}, u32[]{:S(2)}) %collective-permute-start.13) | collective-permute-done | bytes 3145760 | tf_op jit(solution)/shard_map/ppermute | solution.py:48
  559.4 2.0 constant_dynamic-update-slice_fusion.23
  561.4 0.8 collective-permute-start.14
  562.2 132.0 %collective-permute-done.14 = bf16[512,2,24,128]{3,0,2,1:T(8,128)(2,1)S(1)} collective-permute-done((bf16[512,2,24,128]{3,0,2,1:T(8,128)(2,1)S(1)}, bf16[512,2,24,128]{3,0,2,1:T(8,128)(2,1)S(1)}, u32[]{:S(2)}, u32[]{:S(2)}) %collective-permute-start.14) | collective-permute-done | bytes 6291488 | tf_op jit(solution)/shard_map/ppermute | solution.py:48
  694.3 0.8 constant_dynamic-update-slice_fusion.29
  695.1 4.6 copy-done.2
  699.7 1.7 fusion.31
  701.4 0.6 fusion.210
  702.0 10.5 %fusion.211 = (f32[16]{0:T(128)S(1)}, f32[16,3072]{1,0:T(8,128)S(1)}) fusion(bf16[1,24,128,3072]{3,2,1,0:T(8,128)(2,1)} %param.20, bf16[1024,2,24,128]{3,0,2,1:T(8,128)(2,1)} %copy-done.2, f32[24,16]{1,0:T(8,128)S(1)} %fusion.210, f32[24,16,1024]{2,1,0:T(8,128)S(1)} %fusion.31, bf16[16,3072]{1,0:T(8,128)(2,1)S(1)} %get-tuple-element.6), kind=kOutput, calls=%fused_computation.211 | convolution fusion | flops 404620672 | bytes 27035200 | tf_op jit(solution)/shard_map/qhe,hed->qd/dot_general | solution.py:25
  712.5 0.2 multiply_reduce_fusion.3
  712.7 26.5 %fusion.139.clone.1.clone.4 = bf16[16,12288]{1,0:T(8,128)(2,1)S(1)} fusion(bf16[1,3072,12288]{2,1,0:T(8,128)(2,1)} %param.21, f32[16,3072]{1,0:T(8,128)S(1)} %get-tuple-element.52, f32[16]{0:T(128)S(1)} %add_rsqrt_fusion.1, f32[16]{0:T(128)S(1)} %broadcast_multiply_fusion.1), kind=kOutput, calls=%fused_computation.93.clone.clone.clone.clone.clone.1 | convolution fusion | flops 1209876480 | bytes 76087424 | tf_op jit(solution)/shard_map/dot_general | solution.py:27
  739.2 26.3 %fusion.214 = (f32[16]{0:T(128)S(1)}, f32[16,3072]{1,0:T(8,128)S(1)}) fusion(f32[16,3072]{1,0:T(8,128)S(1)} %get-tuple-element.52, bf16[1,12288,3072]{2,1,0:T(8,128)(2,1)} %param.22, bf16[16,12288]{1,0:T(8,128)(2,1)S(1)} %fusion.139.clone.1.clone.4), kind=kOutput, calls=%fused_computation.212 | convolution fusion | flops 1208254464 | bytes 76283968 | tf_op jit(solution)/shard_map/dot_general | solution.py:28
  765.6 0.2 multiply_reduce_fusion.2
  765.8 9.0 %convolution_convert_fusion = bf16[16,3072]{1,0:T(8,128)(2,1)S(1)} fusion(bf16[3072,3072]{1,0:T(8,128)(2,1)} %param.25, f32[16,3072]{1,0:T(8,128)S(1)} %get-tuple-element.54, f32[16]{0:T(128)S(1)} %add_rsqrt_fusion, f32[16]{0:T(128)S(1)} %broadcast_multiply_fusion), kind=kOutput, calls=%fused_computation.52 | convolution fusion | flops 302186496 | bytes 19169408 | tf_op jit(solution)/shard_map/dot_general | solution.py:71
  774.8 1.3 collective-permute-start.15
  776.1 1.2 collective-permute-done.15
  777.2 0.6 fusion.187
  (36 shorter events, 1.5 us)
Async XLA Ops:
  0.0 4.4 copy-start
  0.0 16.1 %copy-start.3 = (bf16[1,8,3072]{2,1,0:T(8,128)(2,1)S(1)}, bf16[1,8,3072]{2,1,0:T(8,128)(2,1)}, u32[]{:S(2)}) copy-start(bf16[1,8,3072]{2,1,0:T(8,128)(2,1)} %param.13) | copy-start | bytes 147460
  0.0 16.1 %collective-permute-start = (bf16[8,3072]{1,0:T(8,128)(2,1)}, bf16[8,3072]{1,0:T(8,128)(2,1)S(1)}, u32[]{:S(2)}, u32[]{:S(2)}) collective-permute-start(bf16[8,3072]{1,0:T(8,128)(2,1)} %bitcast.213), channel_id=1, source_target_pairs={{0,64},{1,65},{2,66},{3,67},{4,68},{5,69},{6,70},{7,71},{8,72},{9,... | collective-permute-start | bytes 147464 | tf_op jit(solution)/shard_map/ppermute | solution.py:57
  13.3 3.9 collective-permute-start.1
  38.5 2.6 collective-permute-start.2
  41.1 10.4 %collective-permute-start.3 = (bf16[32,2,24,128]{3,0,2,1:T(8,128)(2,1)S(1)}, bf16[32,2,24,128]{3,0,2,1:T(8,128)(2,1)S(1)}, u32[]{:S(2)}, u32[]{:S(2)}) collective-permute-start(bf16[32,2,24,128]{3,0,2,1:T(8,128)(2,1)S(1)} %pad_maximum_fusion.4), channel_id=1, source_target_pairs={{0,2},{1,3},{2,0},{3,1},{4,6},{5,7},{6,4},{7,5},{8,10},{9,11},{10,... | collective-permute-start | bytes 1179656 | tf_op jit(solution)/shard_map/ppermute | solution.py:48
  51.6 19.5 %collective-permute-start.4 = (bf16[64,2,24,128]{3,0,2,1:T(8,128)(2,1)S(1)}, bf16[64,2,24,128]{3,0,2,1:T(8,128)(2,1)S(1)}, u32[]{:S(2)}, u32[]{:S(2)}) collective-permute-start(bf16[64,2,24,128]{3,0,2,1:T(8,128)(2,1)S(1)} %pad_maximum_fusion.2), channel_id=1, source_target_pairs={{0,4},{1,5},{2,6},{3,7},{4,0},{5,1},{6,2},{7,3},{8,12},{9,13},{10,... | collective-permute-start | bytes 2359304 | tf_op jit(solution)/shard_map/ppermute | solution.py:48
  71.2 33.7 %collective-permute-start.5 = (bf16[128,2,24,128]{3,0,2,1:T(8,128)(2,1)S(1)}, bf16[128,2,24,128]{3,0,2,1:T(8,128)(2,1)S(1)}, u32[]{:S(2)}, u32[]{:S(2)}) collective-permute-start(bf16[128,2,24,128]{3,0,2,1:T(8,128)(2,1)S(1)} %pad_maximum_fusion), channel_id=1, source_target_pairs={{0,8},{1,9},{2,10},{3,11},{4,12},{5,13},{6,14},{7,15},{8,0},{9,1},... | collective-permute-start | bytes 4718600 | tf_op jit(solution)/shard_map/ppermute | solution.py:48
  107.5 68.0 %collective-permute-start.6 = (bf16[256,2,24,128]{3,0,2,1:T(8,128)(2,1)S(1)}, bf16[256,2,24,128]{3,0,2,1:T(8,128)(2,1)S(1)}, u32[]{:S(2)}, u32[]{:S(2)}) collective-permute-start(bf16[256,2,24,128]{3,0,2,1:T(8,128)(2,1)S(1)} %get-tuple-element.18), channel_id=1, source_target_pairs={{0,16},{1,17},{2,18},{3,19},{4,20},{5,21},{6,22},{7,23},{8,24},{9,... | collective-permute-start | bytes 9437192 | tf_op jit(solution)/shard_map/ppermute | solution.py:48
  179.2 132.9 %collective-permute-start.7 = (bf16[512,2,24,128]{3,0,2,1:T(8,128)(2,1)S(1)}, bf16[512,2,24,128]{3,0,2,1:T(8,128)(2,1)S(1)}, u32[]{:S(2)}, u32[]{:S(2)}) collective-permute-start(bf16[512,2,24,128]{3,0,2,1:T(8,128)(2,1)S(1)} %get-tuple-element.11), channel_id=1, source_target_pairs={{0,32},{1,33},{2,34},{3,35},{4,36},{5,37},{6,38},{7,39},{8,40},{9,... | collective-permute-start | bytes 18874376 | tf_op jit(solution)/shard_map/ppermute | solution.py:48
  390.9 6.9 collective-permute-start.8
  418.6 7.4 collective-permute-start.9
  426.1 10.4 %collective-permute-start.10 = (bf16[32,2,24,128]{3,0,2,1:T(8,128)(2,1)S(1)}, bf16[32,2,24,128]{3,0,2,1:T(8,128)(2,1)S(1)}, u32[]{:S(2)}, u32[]{:S(2)}) collective-permute-start(bf16[32,2,24,128]{3,0,2,1:T(8,128)(2,1)S(1)} %pad_maximum_fusion.5), channel_id=1, source_target_pairs={{0,2},{1,3},{2,0},{3,1},{4,6},{5,7},{6,4},{7,5},{8,10},{9,11},{10,... | collective-permute-start | bytes 1179656 | tf_op jit(solution)/shard_map/ppermute | solution.py:48
  436.6 19.5 %collective-permute-start.11 = (bf16[64,2,24,128]{3,0,2,1:T(8,128)(2,1)S(1)}, bf16[64,2,24,128]{3,0,2,1:T(8,128)(2,1)S(1)}, u32[]{:S(2)}, u32[]{:S(2)}) collective-permute-start(bf16[64,2,24,128]{3,0,2,1:T(8,128)(2,1)S(1)} %pad_maximum_fusion.3), channel_id=1, source_target_pairs={{0,4},{1,5},{2,6},{3,7},{4,0},{5,1},{6,2},{7,3},{8,12},{9,13},{10,... | collective-permute-start | bytes 2359304 | tf_op jit(solution)/shard_map/ppermute | solution.py:48
  456.2 33.7 %collective-permute-start.12 = (bf16[128,2,24,128]{3,0,2,1:T(8,128)(2,1)S(1)}, bf16[128,2,24,128]{3,0,2,1:T(8,128)(2,1)S(1)}, u32[]{:S(2)}, u32[]{:S(2)}) collective-permute-start(bf16[128,2,24,128]{3,0,2,1:T(8,128)(2,1)S(1)} %pad_maximum_fusion.1), channel_id=1, source_target_pairs={{0,8},{1,9},{2,10},{3,11},{4,12},{5,13},{6,14},{7,15},{8,0},{9,1},... | collective-permute-start | bytes 4718600 | tf_op jit(solution)/shard_map/ppermute | solution.py:48
  491.4 68.1 %collective-permute-start.13 = (bf16[256,2,24,128]{3,0,2,1:T(8,128)(2,1)S(1)}, bf16[256,2,24,128]{3,0,2,1:T(8,128)(2,1)S(1)}, u32[]{:S(2)}, u32[]{:S(2)}) collective-permute-start(bf16[256,2,24,128]{3,0,2,1:T(8,128)(2,1)S(1)} %get-tuple-element.15), channel_id=1, source_target_pairs={{0,16},{1,17},{2,18},{3,19},{4,20},{5,21},{6,22},{7,23},{8,24},{9,... | collective-permute-start | bytes 9437192 | tf_op jit(solution)/shard_map/ppermute | solution.py:48
  561.4 132.9 %collective-permute-start.14 = (bf16[512,2,24,128]{3,0,2,1:T(8,128)(2,1)S(1)}, bf16[512,2,24,128]{3,0,2,1:T(8,128)(2,1)S(1)}, u32[]{:S(2)}, u32[]{:S(2)}) collective-permute-start(bf16[512,2,24,128]{3,0,2,1:T(8,128)(2,1)S(1)} %get-tuple-element.9), channel_id=1, source_target_pairs={{0,32},{1,33},{2,34},{3,35},{4,36},{5,37},{6,38},{7,39},{8,40},{9,... | collective-permute-start | bytes 18874376 | tf_op jit(solution)/shard_map/ppermute | solution.py:48
  695.1 4.6 copy-start.2
  765.8 12.1 %copy-start.1 = (bf16[1,8,3072]{2,1,0:T(8,128)(2,1)S(1)}, bf16[1,8,3072]{2,1,0:T(8,128)(2,1)}, u32[]{:S(2)}) copy-start(bf16[1,8,3072]{2,1,0:T(8,128)(2,1)} %param.14) | copy-start | bytes 147460
  774.8 2.5 collective-permute-start.15
where the time goes:
time: 791 us; the launch traced here: 778 us
  waiting for transfers between devices  516 us (65%)
  matrix products  198 us (25%)
  starting transfers between devices  36.2 us (5%)
  local copies, waits for them, and re-layouts  24.7 us (3%)
    ppermute x12, waiting for transfers between devices, gather_kv(): lax.ppermute(gathered, 'branch', perm_list)  508 us
    dot_general x2, matrix products, transformer_block(): jnp.dot(layer_norm(residual), w_up, preferred_element_type=jnp.float32)  52.1 us
    dot_general x2, matrix products, transformer_block(): jnp.dot(hidden, w_down, preferred_element_type=jnp.float32)  51.6 us
    dot_general x2, matrix products, transformer_block(): jnp.dot(layer_norm(residual), w_qkv, preferred_element_type=jnp.float32)  40.2 us
    ppermute x12, starting transfers between devices, gather_kv(): lax.ppermute(gathered, 'branch', perm_list)  26.5 us
    dot_general x2, matrix products, transformer_block(): jnp.einsum('qhe,hed->qd', attn_out, w_proj, preferred_element_type=jnp.fl...  20.7 us
  transfers between devices with their start and end apart: 16, of which 15 were waited for; matrix products, arithmetic and copies ran while one was open for 2% of the time, Pallas kernels for 0%

commit v1 on v0

v1 whole, which is shorter than its diff:
```python
import functools

import jax
import jax.numpy as jnp
from jax import lax
from jax.experimental import pallas as pl
from jax.experimental.pallas import tpu as pltpu
from jax.sharding import PartitionSpec as P

MESH = pl.DeviceIdType.MESH
F32 = jnp.float32
BF16 = jnp.bfloat16
LN_EPS = 1e-6
W = 8
HD = 128
SLOTS = 17

PH_XH, PH_C0, PH_O, PH_U, PH_C1, PH_A1, PH_OT, PH_UT, PH_A2 = 0, 1, 2, 4, 6, 7, 8, 9, 10
NUM_PH = 11
PH_ATT = (PH_O, PH_O + 1, PH_OT)
PH_MID = (PH_U, PH_U + 1, PH_UT)


def normalise(rows):
    centred = rows - jnp.mean(rows, axis=-1, keepdims=True)
    variance = jnp.mean(centred * centred, axis=-1, keepdims=True)
    return (centred * lax.rsqrt(variance + LN_EPS)).astype(BF16)


def add_rounded(a, b):
    return (a.astype(F32) + b.astype(F32)).astype(BF16)


def kernel(n, heads_w, x_ref, h_ref, in_qkv, in_proj, in_up, in_down, tail_qkv, tail_proj, tail_up, tail_down, z_hint, z_out, w_final,
           y_ref, wbuf, wsem, xs, xh, gathered, lnbuf, hid, qkv_out, qkv_in, o_out, part_out, part_in, sum_out, sum_in, sum_own, ystage, ybuf,
           ag_send, ag_recv, qkv_send, qkv_recv, o_send, o_recv, part_send, part_recv, sum_send, sum_recv, y_send, y_recv):
    T = n // W
    R = x_ref.shape[0]
    D = x_ref.shape[1]
    M = W * R
    C = D // W
    FS = hid.shape[1]
    NW1 = FS // C
    scale = HD ** -0.5

    me = lax.axis_index('branch')
    if n == 128:
        c = lax.rem(me, 2)
        x0 = lax.rem(me // 2, 2)
        x1 = lax.rem(me // 4, 2)
        y0 = lax.rem(me // 8, 2)
        y1 = lax.rem(me // 16, 2)
        j = y0 * 2 + x0
        t = (me // 32) * 4 + y1 * 2 + x1
        spread = T // 2
    else:
        c = lax.rem(me, 2)
        j = lax.rem(me, W) // 2
        t = me // W
        spread = 0
    w = j * 2 + c

    def dev(tt, jj, cc):
        if n == 128:
            return (tt // 4) * 32 + lax.rem(tt // 2, 2) * 16 + (jj // 2) * 8 + lax.rem(tt, 2) * 4 + lax.rem(jj, 2) * 2 + cc
        return tt * W + jj * 2 + cc

    def near(r):
        return lax.rem(j // 2 + r // 2, 2) * 2 + lax.rem(lax.rem(j, 2) + lax.rem(r, 2), 2)

    def rcopy(src, dst, ssem, rsem, device):
        return pltpu.make_async_remote_copy(src_ref=src, dst_ref=dst, send_sem=ssem, recv_sem=rsem, device_id={'branch': device}, device_id_type=MESH)

    partner = dev(t, j, 1 - c)

    def cols(ww):
        return pl.ds(pl.multiple_of(ww * C, HD), C)

    chunks = []

    def add(*pieces):
        chunks.append(pieces)
        return len(chunks) - 1

    def columns_of(ref, start):
        return ref.at[:, pl.ds(pl.multiple_of(start, HD), C)]

    def add_qkv(ref):
        return [add(columns_of(ref, p * D + w * C)) for p in (1, 2, 0)][0]

    def add_up(ref):
        return [add(columns_of(ref, w * FS + i * C)) for i in range(NW1)][0]

    def add_down(ref):
        first = len(chunks)
        for core in (1 - c, c):
            for pair in ((1, 2), (3, 0)):
                add(*[ref.at[pl.ds(pl.multiple_of(w * FS, 16), FS), cols(near(r) * 2 + core)] for r in pair])
        return first

    qkv_refs = (in_qkv.at[0], in_qkv.at[1], tail_qkv.at[0])
    proj_refs = (in_proj.at[0], in_proj.at[1], tail_proj.at[0])
    up_refs = (in_up.at[0], in_up.at[1], tail_up.at[0])
    down_refs = (in_down.at[0], in_down.at[1], tail_down.at[0])
    k_hint = add(columns_of(z_hint, w * C))
    k_qkv, k_proj, k_up, k_down = {}, {}, {}, {}
    for b in (0, 1):
        k_qkv[b] = add_qkv(qkv_refs[b])
    for b in (0, 1):
        k_proj[b] = add(columns_of(proj_refs[b], w * C))
    for b in (1, 0):
        k_up[b] = add_up(up_refs[b])
        k_down[b] = add_down(down_refs[b])
    k_zout = add(columns_of(z_out.at[0], w * C))
    k_qkv[2] = add_qkv(qkv_refs[2])
    k_proj[2] = add(columns_of(proj_refs[2], w * C))
    k_up[2] = add_up(up_refs[2])
    k_down[2] = add_down(down_refs[2])
    k_final = add(columns_of(w_final, w * C))

    def fetch(k):
        slot = k % SLOTS
        if len(chunks[k]) == 1:
            pltpu.make_async_copy(chunks[k][0], wbuf.at[slot], wsem.at[slot]).start()
        else:
            for i, piece in enumerate(chunks[k]):
                pltpu.make_async_copy(piece, wbuf.at[slot, pl.ds(i * FS, FS)], wsem.at[slot]).start()

    def ready(slot):
        pltpu.make_async_copy(columns_of(z_hint, 0), wbuf.at[slot], wsem.at[slot]).wait()

    def refill(first, count):
        for k in range(first, first + count):
            if k + SLOTS < len(chunks):
                fetch(k + SLOTS)

    for k in range(min(SLOTS, len(chunks))):
        fetch(k)

    barrier = pltpu.get_barrier_semaphore()

    def greet_group(ww, carry):
        @pl.when(ww != w)
        def _():
            pl.semaphore_signal(barrier, inc=1, device_id={'branch': dev(t, ww // 2, lax.rem(ww, 2))}, device_id_type=MESH)
        return carry

    def greet_tokens(tt, carry):
        @pl.when(tt != t)
        def _():
            pl.semaphore_signal(barrier, inc=1, device_id={'branch': dev(tt, j, c)}, device_id_type=MESH)
        return carry

    lax.fori_loop(0, W, greet_group, 0)
    lax.fori_loop(0, T, greet_tokens, 0)
    xs[w, 0] = x_ref[...]
    xs[w, 1] = h_ref[...]
    pl.semaphore_wait(barrier, W - 1 + T - 1)

    def piece(ph, jj, cc):
        if isinstance(ph, int) and ph == PH_XH:
            return xs.at[jj * 2 + cc]
        return gathered.at[ph - 1, :, cols(jj * 2 + cc)]

    def gather_start(ph):
        own = piece(ph, j, c)
        for r in (3, 1, 2):
            rcopy(own, own, ag_send.at[ph, r], ag_recv.at[ph, r], dev(t, near(r), c)).start()
        rcopy(own, own, ag_send.at[ph, 0], ag_recv.at[ph, 0], partner).start()

    def gather_forward(ph):
        for r in (1, 2, 3):
            got = piece(ph, near(r), c)
            rcopy(got, got, ag_send.at[ph, r], ag_recv.at[ph, r], partner).wait_recv()
            rcopy(got, got, ag_send.at[ph, 3 + r], ag_recv.at[ph, 3 + r], partner).start()

    def gather_finish(ph):
        for r in range(4):
            got = piece(ph, near(r), 1 - c)
            s = 0 if r == 0 else 3 + r
            rcopy(got, got, ag_send.at[ph, s], ag_recv.at[ph, s], partner).wait_recv()

    def gather_drain(ph):
        for s in range(7):
            own = piece(ph, j, c)
            rcopy(own, own, ag_send.at[ph, s], ag_recv.at[ph, s], partner).wait_send()

    def layer_norm(load):
        def rows16(i, carry):
            row = pl.ds(pl.multiple_of(i * 16, 16), 16)
            lnbuf[row, :] = normalise(load(row).astype(F32))
            return carry
        lax.fori_loop(0, M // 16, rows16, 0)

    def matmul(lhs, k):
        slot = k % SLOTS
        ready(slot)
        out = jnp.dot(lhs, wbuf[slot], preferred_element_type=F32)
        return out

    def owner(blk, h):
        return (blk % 2) * heads_w + h + spread * c

    def qkv_block(blk, stage):
        first = k_qkv[blk]

        def part_step(i, carry):
            p = lax.rem(i + 1, 3)
            slot = lax.rem(first + i, SLOTS)
            ready(slot)
            out = jnp.dot(lnbuf[...], wbuf[slot], preferred_element_type=F32).astype(BF16)
            dst_rows = pl.ds(pl.multiple_of(t * M, M), M)
            for h in range(heads_w):
                qkv_out[blk, p, h] = out[:, h * HD:(h + 1) * HD]
            for h in range(heads_w):
                to = owner(blk, h)

                @pl.when(to != t)
                def _():
                    rcopy(qkv_out.at[blk, p, h], qkv_in.at[stage, p, dst_rows], qkv_send.at[blk, p, h], qkv_recv.at[stage, t], dev(to, j, c)).start()

                @pl.when(to == t)
                def _():
                    qkv_in[stage, p, dst_rows, :] = out[:, h * HD:(h + 1) * HD]
            return carry

        lax.fori_loop(0, 3, part_step, 0)
        refill(first, 3)

    def qkv_drain(blk, stage):
        for p in range(3):
            for h in range(heads_w):
                @pl.when(owner(blk, h) != t)
                def _():
                    rcopy(qkv_out.at[blk, p, h], qkv_in.at[stage, p, pl.ds(0, M)], qkv_send.at[blk, p, h], qkv_recv.at[stage, t], partner).wait_send()

    QB = min(128, T * M)
    place = t - spread * c
    owns = (jnp.logical_and(place >= 0, place < 2 * heads_w), jnp.logical_and(place >= 0, place < heads_w))
    own_blk = place // heads_w
    own_head = lax.rem(place, heads_w)

    def attention(stage):
        ph = PH_O + own_blk if stage == 0 else PH_OT
        blk = own_blk if stage == 0 else 2

        @pl.when(owns[stage])
        def _():
            def arrive(tt, carry):
                @pl.when(tt != t)
                def _():
                    slab = qkv_in.at[stage, :, pl.ds(pl.multiple_of(tt * M, M), M)]
                    rcopy(slab, slab, o_send.at[stage, t], qkv_recv.at[stage, tt], partner).wait_recv()
                return carry

            lax.fori_loop(0, T, arrive, 0)

            def queries(i, carry):
                row = pl.ds(pl.multiple_of(i * QB, QB), QB)
                s = lax.dot_general(qkv_in[stage, 0, row, :], qkv_in[stage, 1], (((1,), (1,)), ((), ())), preferred_element_type=F32) * scale
                e = jnp.exp(s - jnp.max(s, axis=-1, keepdims=True))
                p = (e * (1.0 / jnp.sum(e, axis=-1, keepdims=True))).astype(BF16)
                o_out[stage, row, :] = jnp.dot(p, qkv_in[stage, 2], preferred_element_type=F32).astype(BF16)
                for q in range(QB // M):
                    tt = i * (QB // M) + q
                    mine = pl.ds(pl.multiple_of(tt * M, M), M)
                    dst = gathered.at[ph - 1, :, pl.ds(pl.multiple_of(w * C + own_head * HD, HD), HD)]

                    @pl.when(tt != t)
                    def _():
                        rcopy(o_out.at[stage, mine], dst, o_send.at[stage, tt], o_recv.at[blk, own_head], dev(tt, j, c)).start()

                    @pl.when(tt == t)
                    def _():
                        dst[...] = o_out[stage, mine, :]
                return carry

            lax.fori_loop(0, T * M // QB, queries, 0)

    def attention_drain(stage):
        @pl.when(owns[stage])
        def _():
            def left(tt, carry):
                @pl.when(tt != t)
                def _():
                    mine = o_out.at[stage, pl.ds(pl.multiple_of(tt * M, M), M)]
                    rcopy(mine, mine, o_send.at[stage, tt], o_recv.at[0, 0], partner).wait_send()
                return carry
            lax.fori_loop(0, T, left, 0)

    def attention_gather(blk):
        ph = PH_ATT[blk]
        for h in range(heads_w):
            @pl.when(owner(blk, h) != t)
            def _():
                got = gathered.at[ph - 1, :, pl.ds(pl.multiple_of(w * C + h * HD, HD), HD)]
                rcopy(got, got, o_send.at[0, t], o_recv.at[blk, h], partner).wait_recv()
        gather_start(ph)

    def own_cols(blk):
        if blk == 0:
            return xh[0, :, cols(w)]
        return gathered[(PH_C0 if blk == 1 else PH_A1) - 1, :, cols(w)]

    def proj_block(blk):
        ph = PH_ATT[blk]
        gather_forward(ph)
        gather_finish(ph)
        out = matmul(gathered[ph - 1], k_proj[blk]).astype(BF16)
        gathered[PH_MID[blk] - 1, :, cols(w)] = add_rounded(own_cols(blk), out)
        refill(k_proj[blk], 1)
        gather_start(PH_MID[blk])

    def mlp_block(blk):
        ph = PH_MID[blk]
        gather_forward(ph)
        gather_finish(ph)
        layer_norm(lambda row: gathered[ph - 1, row, :])

        def up_step(i, carry):
            slot = lax.rem(k_up[blk] + i, SLOTS)
            ready(slot)
            out = jnp.dot(lnbuf[...], wbuf[slot], preferred_element_type=F32)
            hid[:, pl.ds(pl.multiple_of(i * C, HD), C)] = jax.nn.gelu(out, approximate=True).astype(BF16)
            return carry

        lax.fori_loop(0, NW1, up_step, 0)
        refill(k_up[blk], NW1)

        def down(first, s):
            slot = lax.rem(first + s // 2, SLOTS)

            @pl.when(lax.rem(s, 2) == 0)
            def _():
                ready(slot)
            return jnp.dot(hid[...], wbuf[slot, pl.ds(pl.multiple_of(lax.rem(s, 2) * FS, 16), FS), :], preferred_element_type=F32)

        def for_partner(s, carry):
            part_out[blk, s] = down(k_down[blk], s)
            rcopy(part_out.at[blk, s], part_in.at[blk, s], part_send.at[blk, s], part_recv.at[blk, s], partner).start()
            return carry

        lax.fori_loop(0, 4, for_partner, 0)
        refill(k_down[blk], 2)

        def for_core(s, carry):
            out = down(k_down[blk] + 2, s)
            rcopy(part_out.at[blk, s], part_in.at[blk, s], part_send.at[blk, s], part_recv.at[blk, s], partner).wait_recv()
            out = out + part_in[blk, s]

            @pl.when(s < 3)
            def _():
                sum_out[blk, s] = out
                rcopy(sum_out.at[blk, s], sum_in.at[blk, s], sum_send.at[blk, s], sum_recv.at[blk, s], dev(t, near(s + 1), c)).start()

            @pl.when(s == 3)
            def _():
                sum_own[blk] = out
            return carry

        lax.fori_loop(0, 4, for_core, 0)
        refill(k_down[blk] + 2, 2)

    def mlp_finish(blk):
        total = sum_own[blk]
        for s in range(3):
            rcopy(sum_out.at[blk, s], sum_in.at[blk, s], sum_send.at[blk, s], sum_recv.at[blk, s], partner).wait_recv()
            total = total + sum_in[blk, s]
        return add_rounded(gathered[PH_MID[blk] - 1, :, cols(w)], total.astype(BF16))

    def mlp_drain(blk):
        for s in range(4):
            rcopy(part_out.at[blk, s], part_in.at[blk, s], part_send.at[blk, s], part_recv.at[blk, s], partner).wait_send()
        for s in range(3):
            rcopy(sum_out.at[blk, s], sum_in.at[blk, s], sum_send.at[blk, s], sum_recv.at[blk, s], partner).wait_send()

    gather_start(PH_XH)
    gather_forward(PH_XH)
    gather_finish(PH_XH)
    for which in range(2):
        for i in range(M // 16):
            pair = [xs[16 // R * i + q, which].astype(F32) for q in range(16 // R)]
            xh[which, i * 16:(i + 1) * 16, :] = jnp.concatenate(pair, axis=0).astype(BF16)

    hint = matmul(xh[1], k_hint).astype(BF16)
    refill(k_hint, 1)
    gathered[PH_C0 - 1, :, cols(w)] = add_rounded(xh[0, :, cols(w)], hint)
    gather_start(PH_C0)
    layer_norm(lambda row: xh[0, row, :])
    qkv_block(0, 0)
    gather_forward(PH_C0)
    gather_finish(PH_C0)
    layer_norm(lambda row: gathered[PH_C0 - 1, row, :])
    qkv_block(1, 0)
    attention(0)
    attention_gather(0)
    attention_gather(1)
    proj_block(0)
    proj_block(1)
    mlp_block(1)
    mlp_block(0)
    gathered[PH_C1 - 1, :, cols(w)] = mlp_finish(1)
    gather_start(PH_C1)
    base = mlp_finish(0)
    gather_forward(PH_C1)
    gather_finish(PH_C1)
    resid = matmul(gathered[PH_C1 - 1], k_zout).astype(BF16)
    refill(k_zout, 1)
    gathered[PH_A1 - 1, :, cols(w)] = add_rounded(base, resid)
    gather_start(PH_A1)
    gather_forward(PH_A1)
    gather_finish(PH_A1)
    layer_norm(lambda row: gathered[PH_A1 - 1, row, :])
    qkv_block(2, 1)
    attention(1)
    attention_gather(2)
    proj_block(2)
    mlp_block(2)
    gathered[PH_A2 - 1, :, cols(w)] = mlp_finish(2)
    gather_start(PH_A2)
    gather_forward(PH_A2)
    gather_finish(PH_A2)
    layer_norm(lambda row: gathered[PH_A2 - 1, row, :])
    y = matmul(lnbuf[...], k_final)
    for ww in range(W):
        ystage[ww] = y[ww * R:(ww + 1) * R, :].astype(BF16)

    def y_send_step(ww, carry):
        @pl.when(ww != w)
        def _():
            rcopy(ystage.at[ww], ybuf.at[w], y_send.at[ww], y_recv.at[w], dev(t, ww // 2, lax.rem(ww, 2))).start()

        @pl.when(ww == w)
        def _():
            ybuf[w] = ystage[ww]
        return carry

    lax.fori_loop(0, W, y_send_step, 0)

    def y_recv_step(ww, carry):
        @pl.when(ww != w)
        def _():
            rcopy(ystage.at[ww], ybuf.at[ww], y_send.at[ww], y_recv.at[ww], partner).wait()
        return carry

    lax.fori_loop(0, W, y_recv_step, 0)
    for ww in range(W):
        y_ref[:, ww * C:(ww + 1) * C] = ybuf[ww]

    for ph in range(NUM_PH):
        gather_drain(ph)
    for blk in range(3):
        qkv_drain(blk, blk // 2)
        mlp_drain(blk)
    for stage in range(2):
        attention_drain(stage)


def solution(mesh):
    n = mesh.shape['branch']

    def device_step(x, h, in_qkv, in_proj, in_up, in_down, tail_qkv, tail_proj, tail_up, tail_down, z_hint, z_out, w_final):
        R, D = x.shape[1:]
        heads_w = D // W // HD
        T = n // W
        M = W * R
        C = D // W
        FS = in_up.shape[-1] // W
        vmem = pl.BlockSpec(memory_space=pltpu.VMEM)
        hbm = pl.BlockSpec(memory_space=pl.ANY)
        dma = pltpu.SemaphoreType.DMA
        y = pl.pallas_call(
            functools.partial(kernel, n, heads_w),
            out_shape=jax.ShapeDtypeStruct((R, D), BF16),
            in_specs=[vmem] * 2 + [hbm] * 11,
            out_specs=vmem,
            scratch_shapes=[
                pltpu.VMEM((SLOTS, D, C), BF16),
                dma((SLOTS,)),
                pltpu.VMEM((W, 2, R, D), BF16),
                pltpu.VMEM((2, M, D), BF16),
                pltpu.VMEM((NUM_PH - 1, M, D), BF16),
                pltpu.VMEM((M, D), BF16),
                pltpu.VMEM((M, FS), BF16),
                pltpu.VMEM((3, 3, heads_w, M, HD), BF16),
                pltpu.VMEM((2, 3, T * M, HD), BF16),
                pltpu.VMEM((2, T * M, HD), BF16),
                pltpu.VMEM((3, 4, M, C), F32),
                pltpu.VMEM((3, 4, M, C), F32),
                pltpu.VMEM((3, 3, M, C), F32),
                pltpu.VMEM((3, 3, M, C), F32),
                pltpu.VMEM((3, M, C), F32),
                pltpu.VMEM((W, R, C), BF16),
                pltpu.VMEM((W, R, C), BF16),
                dma((NUM_PH, 7)), dma((NUM_PH, 7)),
                dma((3, 3, heads_w)), dma((2, T)),
                dma((2, T)), dma((3, heads_w)),
                dma((3, 4)), dma((3, 4)),
                dma((3, 3)), dma((3, 3)),
                dma((W,)), dma((W,)),
            ],
            compiler_params=pltpu.CompilerParams(collective_id=0, has_side_effects=True, vmem_limit_bytes=67043328),
        )(
            x[0], h[0], in_qkv[:, 0], in_proj[:, 0].reshape(2, D, D), in_up[:, 0], in_down[:, 0],
            tail_qkv, tail_proj.reshape(1, D, D), tail_up, tail_down, z_hint, z_out, w_final,
        )
        return y[None]

    act_spec = P('data', 'branch', None)
    return jax.shard_map(device_step, mesh=mesh, in_specs=(act_spec, act_spec) + (P(),) * 11, out_specs=act_spec, check_vma=False)
```

time: 791 us -> 132 us (0.17); the launches traced: 778 us -> 131 us
  waiting for transfers between devices: 516 us -> 0 us
  matrix products: 198 us -> 0 us
  Pallas kernels: 0 us -> 130 us
  starting transfers between devices: 36.2 us -> 0 us
  local copies, waits for them, and re-layouts: 24.7 us -> 1.42 us
    ppermute x16 -> x0, waiting for transfers between devices: 516 us -> none  [the longest x12 508 us: gather_kv(): lax.ppermute(gathered, 'branch', perm_list)]
    dot_general x12 -> x0, matrix products: 193 us -> none  [the longest x2 52.1 us: transformer_block(): jnp.dot(layer_norm(residual), w_up, preferred_element_type=jnp.float32)]
    pallas_call x0 -> x1, Pallas kernels: none -> 130 us  [device_step(): pl.pallas_call(functools.partial(kernel, n, heads_w), out_shape=jax.Shape...]
    ppermute x16 -> x0, starting transfers between devices: 36.2 us -> none  [the longest x12 26.5 us: gather_kv(): lax.ppermute(gathered, 'branch', perm_list)]
    unnamed x20 -> x1, local copies, waits for them, and re-layouts: 14.4 us -> 1.42 us
    concatenate x4 -> x0, local copies, waits for them, and re-layouts: 10.3 us -> none  [gather_kv(): jnp.concatenate([gathered, lax.ppermute(gathered, 'branch', perm_list)],...]
  transfers between devices with their start and end apart: 16 -> 0, of which waited for: 15 -> 0; matrix products, arithmetic and copies ran while one was open for 2% -> 0% of each run, Pallas kernels for 0% -> 0%
where the time goes in v1:
time: 132 us; the launch traced here: 131 us
  Pallas kernels  130 us (98%)
  local copies, waits for them, and re-layouts  1.42 us (1%)
    pallas_call x1, Pallas kernels, device_step(): pl.pallas_call(functools.partial(kernel, n, heads_w), out_shape=jax.Shape...  130 us

profile of v1, /device:TPU:1, one launch (start us, length us, event | category | flops | bytes accessed | tf_op | source)
XLA Modules:
  0.0 131.0 jit_solution(5951927139711402447)
XLA Ops:
  0.0 129.5 %shard_map.127 = bf16[8,3072]{1,0:T(8,128)(2,1)} custom-call(bf16[8,3072]{1,0:T(8,128)(2,1)} %bitcast.11, bf16[8,3072]{1,0:T(8,128)(2,1)} %bitcast.12, bf16[2,3072,9216]{2,1,0:T(8,128)(2,1)} %bitcast.2.in_qkv, bf16[2,3072,3072]{2,1,0:T(8,128)(2,1)} %bitcast.8, bf16[2,3072,12288]{2,1,0:T(8,128)(2,1)} %bitcast.4.in_up, ...), custom_call_target="tpu_custom_call" | custom-call | tf_op jit(solution)/shard_map/pallas_call | solution.py:472
  129.5 1.4 %copy.15 = bf16[1,8,3072]{2,1,0:T(8,128)(2,1)} copy(bf16[1,8,3072]{2,1,0:T(8,128)(2,1)} %bitcast.10) | data formatting | bytes 98304

commit v2 on v1

v2 whole, which is shorter than its diff:
```python
import functools

import jax
import jax.numpy as jnp
from jax import lax
from jax.experimental import pallas as pl
from jax.experimental.pallas import tpu as pltpu
from jax.sharding import PartitionSpec as P

MESH = pl.DeviceIdType.MESH
F32 = jnp.float32
BF16 = jnp.bfloat16
LN_EPS = 1e-6
W = 8
HD = 128
SLOTS = 17

FAR_FIRST = (3, 1, 2, 0)

PH_H, PH_X, PH_C1, PH_U2, PH_O = 0, 1, 2, 3, 4
G_C0, G_O, G_U, G_C1, G_U2, G_A1, G_OT, G_UT = 0, 1, 3, 5, 6, 7, 8, 9
NUM_G = 10
G_ATT = (G_O, G_O + 1, G_OT)
G_MID = (G_U, G_U + 1, G_UT)
SH_C0, SH_U, SH_A1 = 0, 1, 4
NUM_SH = 5


def normalise(rows):
    centred = rows - jnp.mean(rows, axis=-1, keepdims=True)
    variance = jnp.mean(centred * centred, axis=-1, keepdims=True)
    return (centred * lax.rsqrt(variance + LN_EPS)).astype(BF16)


def add_rounded(a, b):
    return (a.astype(F32) + b.astype(F32)).astype(BF16)


def kernel(n, heads_w, x_ref, h_ref, in_qkv, in_proj, in_up, in_down, tail_qkv, tail_proj, tail_up, tail_down, z_hint, z_out, w_final,
           y_ref, wbuf, wsem, xs, xh, gathered, lnbuf, lnrow, hid, qkv_out, qkv_in, o_out, sum_out, sum_in, sum_own, row_out, row_in,
           ag_send, ag_recv, sh_send, sh_recv, qkv_send, qkv_recv, o_send, o_recv, hid_send, hid_recv, sum_send, sum_recv, row_send, row_recv):
    T = n // W
    R = x_ref.shape[0]
    D = x_ref.shape[1]
    M = W * R
    C = D // W
    FS = hid.shape[2] // 2
    NW1 = FS // C
    scale = HD ** -0.5 * 1.4426950408889634

    me = lax.axis_index('branch')
    if n == 128:
        c = lax.rem(me, 2)
        x0 = lax.rem(me // 2, 2)
        x1 = lax.rem(me // 4, 2)
        y0 = lax.rem(me // 8, 2)
        y1 = lax.rem(me // 16, 2)
        j = y0 * 2 + x0
        t = (me // 32) * 4 + y1 * 2 + x1
    else:
        c = lax.rem(me, 2)
        j = lax.rem(me, W) // 2
        t = me // W
    w = j * 2 + c

    def dev(tt, jj, cc):
        if n == 128:
            return (tt // 4) * 32 + lax.rem(tt // 2, 2) * 16 + (jj // 2) * 8 + lax.rem(tt, 2) * 4 + lax.rem(jj, 2) * 2 + cc
        return tt * W + jj * 2 + cc

    def near(r):
        return lax.rem(j // 2 + r // 2, 2) * 2 + lax.rem(lax.rem(j, 2) + lax.rem(r, 2), 2)

    def rcopy(src, dst, ssem, rsem, device):
        return pltpu.make_async_remote_copy(src_ref=src, dst_ref=dst, send_sem=ssem, recv_sem=rsem, device_id={'branch': device}, device_id_type=MESH)

    partner = dev(t, j, 1 - c)

    def cols(ww):
        return pl.ds(pl.multiple_of(ww * C, HD), C)

    def head_cols(ww, h):
        return pl.ds(pl.multiple_of(ww * C + h * HD, HD), HD)

    chunks = []

    def add(source):
        chunks.append(source)
        return len(chunks) - 1

    def columns_of(ref, start):
        return ref.at[:, pl.ds(pl.multiple_of(start, HD), C)]

    def add_qkv(ref):
        return [add(columns_of(ref, p * D + w * C)) for p in (1, 2, 0)][0]

    def add_up(ref):
        return [add(columns_of(ref, w * FS + i * C)) for i in range(NW1)][0]

    def add_slices(ref):
        return [add(columns_of(ref, (near(r) * 2 + c) * C)) for r in range(4)][0]

    def add_down(ref, starts):
        return [add(ref.at[pl.ds(pl.multiple_of(j * 2 * FS, 16), 2 * FS), pl.ds(pl.multiple_of(start, HD), C)]) for start in starts][0]

    qkv_refs = (in_qkv.at[0], in_qkv.at[1], tail_qkv.at[0])
    proj_refs = (in_proj.at[0], in_proj.at[1], tail_proj.at[0])
    up_refs = (in_up.at[0], in_up.at[1], tail_up.at[0])
    down_refs = (in_down.at[0], in_down.at[1], tail_down.at[0])
    k_qkv, k_proj, k_up, k_down = {}, {}, {}, {}
    k_hint = add_slices(z_hint)
    for b in (0, 1):
        k_qkv[b] = add_qkv(qkv_refs[b])
    for b in (0, 1):
        k_proj[b] = add_slices(proj_refs[b])
    for b in (1, 0):
        k_up[b] = add_up(up_refs[b])
    for b in (1, 0):
        k_down[b] = add_down(down_refs[b], [(near(r) * 2 + c) * C for r in FAR_FIRST])
    k_zout = add_slices(z_out.at[0])
    k_qkv[2] = add_qkv(qkv_refs[2])
    k_proj[2] = add_slices(proj_refs[2])
    k_up[2] = add_up(up_refs[2])
    k_down[2] = add_down(down_refs[2], [(4 * c + m) * C for m in range(4)])
    k_final = [add(columns_of(w_final, m * C)) for m in range(W)][0]

    def fetch(k):
        pltpu.make_async_copy(chunks[k], wbuf.at[k % SLOTS], wsem.at[k % SLOTS]).start()

    def ready(slot):
        pltpu.make_async_copy(columns_of(z_hint, 0), wbuf.at[slot], wsem.at[slot]).wait()

    def refill(first, count):
        for k in range(first, first + count):
            if k + SLOTS < len(chunks):
                fetch(k + SLOTS)

    for k in range(min(SLOTS, len(chunks))):
        fetch(k)

    barrier = pltpu.get_barrier_semaphore()

    def greet_group(ww, carry):
        @pl.when(ww != w)
        def _():
            pl.semaphore_signal(barrier, inc=1, device_id={'branch': dev(t, ww // 2, lax.rem(ww, 2))}, device_id_type=MESH)
        return carry

    def greet_tokens(tt, carry):
        @pl.when(tt != t)
        def _():
            pl.semaphore_signal(barrier, inc=1, device_id={'branch': dev(tt, j, c)}, device_id_type=MESH)
        return carry

    lax.fori_loop(0, W, greet_group, 0)
    lax.fori_loop(0, T, greet_tokens, 0)
    xs[PH_H, w] = h_ref[...]
    xs[PH_X, w] = x_ref[...]
    pl.semaphore_wait(barrier, W - 1 + T - 1)

    landing = {PH_C1: G_C1, PH_U2: G_U2}
    num_ph = PH_O + 3 * heads_w

    def att_phases(blk):
        return range(PH_O + blk * heads_w, PH_O + (blk + 1) * heads_w)

    def piece(ph, jj, cc):
        if ph in (PH_H, PH_X):
            return xs.at[ph, jj * 2 + cc]
        if ph >= PH_O:
            return gathered.at[G_ATT[(ph - PH_O) // heads_w], :, head_cols(jj * 2 + cc, (ph - PH_O) % heads_w)]
        return gathered.at[landing[ph], :, cols(jj * 2 + cc)]

    def gather_start(ph):
        own = piece(ph, j, c)
        for r in (3, 1, 2):
            rcopy(own, own, ag_send.at[ph, r], ag_recv.at[ph, r], dev(t, near(r), c)).start()
        if ph != PH_U2:
            rcopy(own, own, ag_send.at[ph, 0], ag_recv.at[ph, 0], partner).start()

    def gather_forward(ph):
        for r in (1, 2, 3):
            got = piece(ph, near(r), c)
            rcopy(got, got, ag_send.at[ph, r], ag_recv.at[ph, r], partner).wait_recv()
            rcopy(got, got, ag_send.at[ph, 3 + r], ag_recv.at[ph, 3 + r], partner).start()

    def gather_finish(ph):
        for r in range(4):
            got = piece(ph, near(r), 1 - c)
            s = 0 if r == 0 else 3 + r
            rcopy(got, got, ag_send.at[ph, s], ag_recv.at[ph, s], partner).wait_recv()

    def gather_drain(ph):
        for s in range(7) if ph != PH_U2 else (1, 2, 3):
            own = piece(ph, j, c)
            rcopy(own, own, ag_send.at[ph, s], ag_recv.at[ph, s], partner).wait_send()

    def layer_norm(load):
        for i in range(M // 16):
            lnbuf[i * 16:(i + 1) * 16, :] = normalise(load(slice(i * 16, (i + 1) * 16)).astype(F32))

    def matmul(lhs, k):
        ready(k % SLOTS)
        return jnp.dot(lhs, wbuf[k % SLOTS], preferred_element_type=F32)

    def shared_dots(lhs, first, dst, lo, hi):
        def slice_step(r, carry):
            slot = lax.rem(first + r, SLOTS)
            ready(slot)
            gathered[dst, :, cols(near(r) * 2 + c)] = jnp.dot(lhs[...], wbuf[slot], preferred_element_type=F32).astype(BF16)
            return carry

        lax.fori_loop(lo, hi, slice_step, 0)
        refill(first + lo, hi - lo)

    def hand_over(dst, sh, r):
        handed = gathered.at[dst, :, cols(near(r) * 2 + c)]
        rcopy(handed, handed, sh_send.at[sh, r], sh_recv.at[sh, r], partner).start()

    def shared_add(residual, dst, sh, awaited=None):
        for r in range(4):
            mine = cols(near(r) * 2 + c)
            if awaited is not None and r > 0:
                got = piece(awaited, near(r), c)
                rcopy(got, got, ag_send.at[awaited, r], ag_recv.at[awaited, r], partner).wait_recv()
            gathered[dst, :, mine] = add_rounded(residual[:, mine], gathered[dst, :, mine])
            hand_over(dst, sh, r)

    def shared_matmul(lhs, first, residual, dst, sh):
        def slice_step(r, carry):
            slot = lax.rem(first + r, SLOTS)
            mine = cols(near(r) * 2 + c)
            ready(slot)
            out = jnp.dot(lhs[...], wbuf[slot], preferred_element_type=F32).astype(BF16)
            gathered[dst, :, mine] = add_rounded(residual[:, mine], out)
            hand_over(dst, sh, r)
            return carry

        lax.fori_loop(0, 4, slice_step, 0)
        refill(first, 4)

    def shared_finish(dst, sh):
        for r in range(4):
            got = gathered.at[dst, :, cols(near(r) * 2 + 1 - c)]
            rcopy(got, got, sh_send.at[sh, r], sh_recv.at[sh, r], partner).wait_recv()

    def shared_drain(sh):
        for r in range(4):
            own = gathered.at[0, :, cols(w)]
            rcopy(own, own, sh_send.at[sh, r], sh_recv.at[sh, r], partner).wait_send()

    def owner(blk, h):
        if n == 128:
            return (1 - c if blk == 0 else 2 + c) * 4 + h + 1
        return blk % 2 * heads_w + h

    def qkv_block(blk, stage):
        first = k_qkv[blk]

        def part_step(i, carry):
            p = lax.rem(i + 1, 3)
            slot = lax.rem(first + i, SLOTS)
            ready(slot)
            out = jnp.dot(lnbuf[...], wbuf[slot], preferred_element_type=F32).astype(BF16)
            dst_rows = pl.ds(pl.multiple_of(t * M, M), M)
            for h in range(heads_w):
                qkv_out[blk, p, h] = out[:, h * HD:(h + 1) * HD]
            for h in range(heads_w):
                to = owner(blk, h)

                @pl.when(to != t)
                def _():
                    rcopy(qkv_out.at[blk, p, h], qkv_in.at[stage, p, dst_rows], qkv_send.at[blk, p, h], qkv_recv.at[stage, t], dev(to, j, c)).start()

                @pl.when(to == t)
                def _():
                    qkv_in[stage, p, dst_rows, :] = out[:, h * HD:(h + 1) * HD]
            return carry

        lax.fori_loop(0, 3, part_step, 0)
        refill(first, 3)

    def qkv_drain(blk, stage):
        for p in range(3):
            for h in range(heads_w):
                @pl.when(owner(blk, h) != t)
                def _():
                    rcopy(qkv_out.at[blk, p, h], qkv_in.at[stage, p, pl.ds(0, M)], qkv_send.at[blk, p, h], qkv_recv.at[stage, t], partner).wait_send()

    QB = min(512, T * M)
    QH = QB // 2
    if n == 128:
        last = jnp.logical_and(t // 4 == 2 + c, lax.rem(t, 4) > 0)
        first_blk = jnp.logical_and(t // 4 == 1 - c, lax.rem(t, 4) > 0)
        owns = (jnp.logical_or(first_blk, last), last)
        own_blk = t // 8
        own_head = jnp.maximum(lax.rem(t, 4) - 1, 0)
    else:
        owns = (t < 2 * heads_w, t < heads_w)
        own_blk = t // heads_w
        own_head = lax.rem(t, heads_w)

    def attention(stage):
        land = G_O + own_blk if stage == 0 else G_OT
        blk = own_blk if stage == 0 else 2

        @pl.when(owns[stage])
        def _():
            def arrive(tt, carry):
                @pl.when(tt != t)
                def _():
                    slab = qkv_in.at[stage, :, pl.ds(pl.multiple_of(tt * M, M), M)]
                    rcopy(slab, slab, o_send.at[stage, t], qkv_recv.at[stage, tt], partner).wait_recv()
                return carry

            lax.fori_loop(0, T, arrive, 0)

            def queries(i, carry):
                rows = [pl.ds(pl.multiple_of(i * QB + g * QH, QH), QH) for g in range(2)]
                scores = [lax.dot_general(qkv_in[stage, 0, row, :], qkv_in[stage, 1], (((1,), (1,)), ((), ())), preferred_element_type=F32) for row in rows]
                for row, s in zip(rows, scores):
                    e = jnp.exp2((s - jnp.max(s, axis=-1, keepdims=True)) * scale)
                    p = (e * (1.0 / jnp.sum(e, axis=-1, keepdims=True))).astype(BF16)
                    o_out[stage, row, :] = jnp.dot(p, qkv_in[stage, 2], preferred_element_type=F32).astype(BF16)
                for q in range(QB // M):
                    tt = i * (QB // M) + q
                    mine = pl.ds(pl.multiple_of(tt * M, M), M)
                    dst = gathered.at[land, :, head_cols(w, own_head)]

                    @pl.when(tt != t)
                    def _():
                        rcopy(o_out.at[stage, mine], dst, o_send.at[stage, tt], o_recv.at[blk, own_head], dev(tt, j, c)).start()

                    @pl.when(tt == t)
                    def _():
                        dst[...] = o_out[stage, mine, :]
                return carry

            lax.fori_loop(0, T * M // QB, queries, 0)

    def attention_drain(stage):
        @pl.when(owns[stage])
        def _():
            def left(tt, carry):
                @pl.when(tt != t)
                def _():
                    mine = o_out.at[stage, pl.ds(pl.multiple_of(tt * M, M), M)]
                    rcopy(mine, mine, o_send.at[stage, tt], o_recv.at[0, 0], partner).wait_send()
                return carry
            lax.fori_loop(0, T, left, 0)

    def attention_gather(blk):
        for h, ph in enumerate(att_phases(blk)):
            @pl.when(owner(blk, h) != t)
            def _():
                got = piece(ph, j, c)
                rcopy(got, got, o_send.at[0, t], o_recv.at[blk, h], partner).wait_recv()
            gather_start(ph)

    def proj_block(blk):
        residual = (xh.at[PH_X], gathered.at[G_C0], gathered.at[G_A1])[blk]
        for ph in att_phases(blk):
            gather_forward(ph)
        for ph in att_phases(blk):
            gather_finish(ph)
        shared_matmul(gathered.at[G_ATT[blk]], k_proj[blk], residual, G_MID[blk], SH_U + blk)

    def up_block(blk):
        shared_finish(G_MID[blk], SH_U + blk)
        layer_norm(lambda row: gathered[G_MID[blk], row, :])

        def up_step(i, carry):
            slot = lax.rem(k_up[blk] + i, SLOTS)
            ready(slot)
            out = jnp.dot(lnbuf[...], wbuf[slot], preferred_element_type=F32)
            mine = pl.ds(pl.multiple_of(c * FS + i * C, HD), C)
            hid[blk, :, mine] = jax.nn.gelu(out, approximate=True).astype(BF16)
            rcopy(hid.at[blk, :, mine], hid.at[blk, :, mine], hid_send.at[blk, i], hid_recv.at[blk, i], partner).start()
            return carry

        lax.fori_loop(0, NW1, up_step, 0)
        refill(k_up[blk], NW1)

    def hidden_ready(blk):
        for i in range(NW1):
            got = hid.at[blk, :, pl.ds(pl.multiple_of((1 - c) * FS + i * C, HD), C)]
            rcopy(got, got, hid_send.at[blk, i], hid_recv.at[blk, i], partner).wait_recv()

    def hidden_drain(blk):
        for i in range(NW1):
            got = hid.at[blk, :, pl.ds(pl.multiple_of(c * FS + i * C, HD), C)]
            rcopy(got, got, hid_send.at[blk, i], hid_recv.at[blk, i], partner).wait_send()

    def down_block(blk):
        hidden_ready(blk)
        for s, r in enumerate(FAR_FIRST):
            out = matmul(hid[blk], k_down[blk] + s)
            if r == 0:
                sum_own[blk] = out
            else:
                sum_out[blk, r - 1] = out
                rcopy(sum_out.at[blk, r - 1], sum_in.at[blk, r - 1], sum_send.at[blk, r - 1], sum_recv.at[blk, r - 1], dev(t, near(r), c)).start()
        refill(k_down[blk], 4)

    def down_finish(blk):
        total = sum_own[blk]
        for s in range(3):
            rcopy(sum_out.at[blk, s], sum_in.at[blk, s], sum_send.at[blk, s], sum_recv.at[blk, s], partner).wait_recv()
            total = total + sum_in[blk, s]
        return add_rounded(gathered[G_MID[blk], :, cols(w)], total.astype(BF16))

    def down_drain(blk):
        for s in range(3):
            rcopy(sum_out.at[blk, s], sum_in.at[blk, s], sum_send.at[blk, s], sum_recv.at[blk, s], partner).wait_send()

    def down_rows():
        def half_dot(m, core):
            part = pl.ds(pl.multiple_of(core * FS, HD), FS)
            return jnp.dot(hid[2, :, part], wbuf[(k_down[2] + m) % SLOTS, part, :], preferred_element_type=F32)

        for m in range(4):
            span = slice(m * C, (m + 1) * C)
            if m < 2:
                ready((k_down[2] + m) % SLOTS)
                row_out[:, span] = half_dot(m, c)
        hidden_ready(2)
        for m in range(4):
            span = slice(m * C, (m + 1) * C)
            row_out[:, span] = row_out[:, span] + half_dot(m, 1 - c) if m < 2 else matmul(hid[2], k_down[2] + m)
            for r in FAR_FIRST:
                for cc in ((c, 1 - c) if r else (1 - c,)):
                    to = near(r) * 2 + cc
                    out = row_out.at[pl.ds(pl.multiple_of(to * R, R), R), span]
                    rcopy(out, row_in.at[w, :, span], row_send.at[m, to], row_recv.at[m, w], dev(t, near(r), cc)).start()
        refill(k_down[2], 4)

    def rows_finish():
        def arrive(ww, carry):
            @pl.when(ww != w)
            def _():
                for m in range(4):
                    got = row_in.at[ww, :, m * C:(m + 1) * C]
                    rcopy(got, got, row_send.at[m, ww], row_recv.at[m, ww], partner).wait()
            return carry

        lax.fori_loop(0, W, arrive, 0)
        row_in[w] = row_out[pl.ds(pl.multiple_of(w * R, R), R), :]
        sums = []
        for cc in range(2):
            total = row_in[cc]
            for jj in range(1, 4):
                total = total + row_in[jj * 2 + cc]
            sums.append(total.astype(BF16))
        both = gathered[G_UT, pl.ds(pl.multiple_of(w // 2 * 2 * R, 2 * R), 2 * R), :].astype(F32)
        residual = jnp.where(c == 0, both[:R], both[R:])
        return (residual + jnp.concatenate(sums, axis=1).astype(F32)).astype(BF16)

    def unpack(ph):
        for i in range(M // 16):
            rows = [xs[ph, 16 // R * i + q].astype(F32) for q in range(16 // R)]
            xh[ph, i * 16:(i + 1) * 16, :] = jnp.concatenate(rows, axis=0).astype(BF16)

    gather_start(PH_H)
    gather_start(PH_X)
    gather_forward(PH_H)
    gather_finish(PH_H)
    unpack(PH_H)
    shared_dots(xh.at[PH_H], k_hint, G_C0, 0, 2)
    gather_forward(PH_X)
    shared_dots(xh.at[PH_H], k_hint, G_C0, 2, 4)
    gather_finish(PH_X)
    unpack(PH_X)
    shared_add(xh.at[PH_X], G_C0, SH_C0)
    layer_norm(lambda row: xh[PH_X, row, :])
    qkv_block(0, 0)
    shared_finish(G_C0, SH_C0)
    layer_norm(lambda row: gathered[G_C0, row, :])
    qkv_block(1, 0)
    attention(0)
    attention_gather(0)
    attention_gather(1)
    proj_block(0)
    proj_block(1)
    up_block(1)
    up_block(0)
    down_block(1)
    down_block(0)
    gathered[G_C1, :, cols(w)] = down_finish(1)
    gather_start(PH_C1)
    gather_forward(PH_C1)
    gathered[G_U2, :, cols(w)] = down_finish(0)
    gather_start(PH_U2)
    gather_finish(PH_C1)
    shared_dots(gathered.at[G_C1], k_zout, G_A1, 0, 4)
    shared_add(gathered.at[G_U2], G_A1, SH_A1, PH_U2)
    shared_finish(G_A1, SH_A1)
    layer_norm(lambda row: gathered[G_A1, row, :])
    qkv_block(2, 1)
    attention(1)
    attention_gather(2)
    proj_block(2)
    up_block(2)
    down_rows()
    lnrow[...] = normalise(rows_finish().astype(F32))

    def final_step(m, carry):
        slot = lax.rem(k_final + m, SLOTS)
        ready(slot)
        out = jnp.dot(lnrow[...], wbuf[slot], preferred_element_type=F32)
        y_ref[:, pl.ds(pl.multiple_of(m * C, HD), C)] = out.astype(BF16)
        return carry

    lax.fori_loop(0, W, final_step, 0)

    for ph in range(num_ph):
        gather_drain(ph)
    for sh in range(NUM_SH):
        shared_drain(sh)
    for blk in range(3):
        qkv_drain(blk, blk // 2)
        hidden_drain(blk)
    for blk in range(2):
        down_drain(blk)
    for stage in range(2):
        attention_drain(stage)


def solution(mesh):
    n = mesh.shape['branch']

    def device_step(x, h, in_qkv, in_proj, in_up, in_down, tail_qkv, tail_proj, tail_up, tail_down, z_hint, z_out, w_final):
        R, D = x.shape[1:]
        heads_w = D // W // HD
        T = n // W
        M = W * R
        C = D // W
        FS = in_up.shape[-1] // W
        vmem = pl.BlockSpec(memory_space=pltpu.VMEM)
        hbm = pl.BlockSpec(memory_space=pl.ANY)
        dma = pltpu.SemaphoreType.DMA
        y = pl.pallas_call(
            functools.partial(kernel, n, heads_w),
            out_shape=jax.ShapeDtypeStruct((R, D), BF16),
            in_specs=[vmem] * 2 + [hbm] * 11,
            out_specs=vmem,
            scratch_shapes=[
                pltpu.VMEM((SLOTS, D, C), BF16),
                dma((SLOTS,)),
                pltpu.VMEM((2, W, R, D), BF16),
                pltpu.VMEM((2, M, D), BF16),
                pltpu.VMEM((NUM_G, M, D), BF16),
                pltpu.VMEM((M, D), BF16),
                pltpu.VMEM((R, D), BF16),
                pltpu.VMEM((3, M, 2 * FS), BF16),
                pltpu.VMEM((3, 3, heads_w, M, HD), BF16),
                pltpu.VMEM((2, 3, T * M, HD), BF16),
                pltpu.VMEM((2, T * M, HD), BF16),
                pltpu.VMEM((2, 3, M, C), F32),
                pltpu.VMEM((2, 3, M, C), F32),
                pltpu.VMEM((2, M, C), F32),
                pltpu.VMEM((M, D // 2), F32),
                pltpu.VMEM((W, R, D // 2), F32),
                dma((PH_O + 3 * heads_w, 7)), dma((PH_O + 3 * heads_w, 7)),
                dma((NUM_SH, 4)), dma((NUM_SH, 4)),
                dma((3, 3, heads_w)), dma((2, T)),
                dma((2, T)), dma((3, heads_w)),
                dma((3, FS // C)), dma((3, FS // C)),
                dma((2, 3)), dma((2, 3)),
                dma((4, W)), dma((4, W)),
            ],
            compiler_params=pltpu.CompilerParams(collective_id=0, has_side_effects=True, vmem_limit_bytes=67043328),
        )(
            x[0], h[0], in_qkv[:, 0], in_proj[:, 0].reshape(2, D, D), in_up[:, 0], in_down[:, 0],
            tail_qkv, tail_proj.reshape(1, D, D), tail_up, tail_down, z_hint, z_out, w_final,
        )
        return y[None]

    act_spec = P('data', 'branch', None)
    return jax.shard_map(device_step, mesh=mesh, in_specs=(act_spec, act_spec) + (P(),) * 11, out_specs=act_spec, check_vma=False)
```

time: 132 us -> 113 us (0.86)
  Pallas kernels: 130 us -> 112 us
    pallas_call x1, Pallas kernels: 130 us -> 112 us  [device_step(): pl.pallas_call(functools.partial(kernel, n, heads_w), out_shape=jax.Shape...]
where the time goes in v2:
time: 113 us
  Pallas kernels  112 us (99%)
  local copies, waits for them, and re-layouts  1.42 us (1%)
    pallas_call x1, Pallas kernels, device_step(): pl.pallas_call(functools.partial(kernel, n, heads_w), out_shape=jax.Shape...  112 us

profile of v2, /device:TPU:1, one launch (start us, length us, event | category | flops | bytes accessed | tf_op | source)
XLA Modules:
  0.0 113.2 jit_solution(16462676038457551921)
XLA Ops:
  0.0 111.7 %shard_map.127 = bf16[8,3072]{1,0:T(8,128)(2,1)} custom-call(bf16[8,3072]{1,0:T(8,128)(2,1)} %bitcast.11, bf16[8,3072]{1,0:T(8,128)(2,1)} %bitcast.12, bf16[2,3072,9216]{2,1,0:T(8,128)(2,1)} %bitcast.2.in_qkv, bf16[2,3072,3072]{2,1,0:T(8,128)(2,1)} %bitcast.8, bf16[2,3072,12288]{2,1,0:T(8,128)(2,1)} %bitcast.4.in_up, ...), custom_call_target="tpu_custom_call" | custom-call | tf_op jit(solution)/shard_map/pallas_call | solution.py:541
  111.7 1.4 %copy.15 = bf16[1,8,3072]{2,1,0:T(8,128)(2,1)} copy(bf16[1,8,3072]{2,1,0:T(8,128)(2,1)} %bitcast.10) | data formatting | bytes 98304

commit v3 on v2

--- a/solution.py
+++ b/solution.py
@@ -17,9 +17,11 @@
 
 FAR_FIRST = (3, 1, 2, 0)
 
-PH_H, PH_X, PH_C1, PH_U2, PH_O = 0, 1, 2, 3, 4
+PH_H, PH_X, PH_O, PH_C1, PH_OT, PH_U2 = 0, 1, 2, 4, 5, 6
+NUM_PH = 7
 G_C0, G_O, G_U, G_C1, G_U2, G_A1, G_OT, G_UT = 0, 1, 3, 5, 6, 7, 8, 9
 NUM_G = 10
+PH_ATT = (PH_O, PH_O + 1, PH_OT)
 G_ATT = (G_O, G_O + 1, G_OT)
 G_MID = (G_U, G_U + 1, G_UT)
 SH_C0, SH_U, SH_A1 = 0, 1, 4
@@ -57,10 +59,12 @@
         y1 = lax.rem(me // 16, 2)
         j = y0 * 2 + x0
         t = (me // 32) * 4 + y1 * 2 + x1
+        spread = T // 2
     else:
         c = lax.rem(me, 2)
         j = lax.rem(me, W) // 2
         t = me // W
+        spread = 0
     w = j * 2 + c
 
     def dev(tt, jj, cc):
@@ -78,9 +82,6 @@
 
     def cols(ww):
         return pl.ds(pl.multiple_of(ww * C, HD), C)
-
-    def head_cols(ww, h):
-        return pl.ds(pl.multiple_of(ww * C + h * HD, HD), HD)
 
     chunks = []
 
@@ -115,7 +116,6 @@
         k_proj[b] = add_slices(proj_refs[b])
     for b in (1, 0):
         k_up[b] = add_up(up_refs[b])
-    for b in (1, 0):
         k_down[b] = add_down(down_refs[b], [(near(r) * 2 + c) * C for r in FAR_FIRST])
     k_zout = add_slices(z_out.at[0])
     k_qkv[2] = add_qkv(qkv_refs[2])
@@ -158,17 +158,11 @@
     xs[PH_X, w] = x_ref[...]
     pl.semaphore_wait(barrier, W - 1 + T - 1)
 
-    landing = {PH_C1: G_C1, PH_U2: G_U2}
-    num_ph = PH_O + 3 * heads_w
-
-    def att_phases(blk):
-        return range(PH_O + blk * heads_w, PH_O + (blk + 1) * heads_w)
+    landing = {PH_O: G_O, PH_O + 1: G_O + 1, PH_C1: G_C1, PH_OT: G_OT, PH_U2: G_U2}
 
     def piece(ph, jj, cc):
         if ph in (PH_H, PH_X):
             return xs.at[ph, jj * 2 + cc]
-        if ph >= PH_O:
-            return gathered.at[G_ATT[(ph - PH_O) // heads_w], :, head_cols(jj * 2 + cc, (ph - PH_O) % heads_w)]
         return gathered.at[landing[ph], :, cols(jj * 2 + cc)]
 
     def gather_start(ph):
@@ -203,6 +197,25 @@
         ready(k % SLOTS)
         return jnp.dot(lhs, wbuf[k % SLOTS], preferred_element_type=F32)
 
+    def shared_matmul(lhs, first, residual, dst, sh, awaited=None):
+        def slice_step(r, carry):
+            slot = lax.rem(first + r, SLOTS)
+            mine = cols(near(r) * 2 + c)
+            ready(slot)
+            out = jnp.dot(lhs[...], wbuf[slot], preferred_element_type=F32).astype(BF16)
+            if awaited is not None:
+                @pl.when(r > 0)
+                def _():
+                    got = piece(awaited, near(r), c)
+                    rcopy(got, got, ag_send.at[awaited, r], ag_recv.at[awaited, r], partner).wait_recv()
+            gathered[dst, :, mine] = add_rounded(residual[:, mine], out)
+            handed = gathered.at[dst, :, mine]
+            rcopy(handed, handed, sh_send.at[sh, r], sh_recv.at[sh, r], partner).start()
+            return carry
+
+        lax.fori_loop(0, 4, slice_step, 0)
+        refill(first, 4)
+
     def shared_dots(lhs, first, dst, lo, hi):
         def slice_step(r, carry):
             slot = lax.rem(first + r, SLOTS)
@@ -213,31 +226,12 @@
         lax.fori_loop(lo, hi, slice_step, 0)
         refill(first + lo, hi - lo)
 
-    def hand_over(dst, sh, r):
-        handed = gathered.at[dst, :, cols(near(r) * 2 + c)]
-        rcopy(handed, handed, sh_send.at[sh, r], sh_recv.at[sh, r], partner).start()
-
-    def shared_add(residual, dst, sh, awaited=None):
+    def shared_add(residual, dst, sh):
         for r in range(4):
             mine = cols(near(r) * 2 + c)
-            if awaited is not None and r > 0:
-                got = piece(awaited, near(r), c)
-                rcopy(got, got, ag_send.at[awaited, r], ag_recv.at[awaited, r], partner).wait_recv()
             gathered[dst, :, mine] = add_rounded(residual[:, mine], gathered[dst, :, mine])
-            hand_over(dst, sh, r)
-
-    def shared_matmul(lhs, first, residual, dst, sh):
-        def slice_step(r, carry):
-            slot = lax.rem(first + r, SLOTS)
-            mine = cols(near(r) * 2 + c)
-            ready(slot)
-            out = jnp.dot(lhs[...], wbuf[slot], preferred_element_type=F32).astype(BF16)
-            gathered[dst, :, mine] = add_rounded(residual[:, mine], out)
-            hand_over(dst, sh, r)
-            return carry
-
-        lax.fori_loop(0, 4, slice_step, 0)
-        refill(first, 4)
+            handed = gathered.at[dst, :, mine]
+            rcopy(handed, handed, sh_send.at[sh, r], sh_recv.at[sh, r], partner).start()
 
     def shared_finish(dst, sh):
         for r in range(4):
@@ -250,9 +244,7 @@
             rcopy(own, own, sh_send.at[sh, r], sh_recv.at[sh, r], partner).wait_send()
 
     def owner(blk, h):
-        if n == 128:
-            return (1 - c if blk == 0 else 2 + c) * 4 + h + 1
-        return blk % 2 * heads_w + h
+        return (blk % 2) * heads_w + h + spread * c
 
     def qkv_block(blk, stage):
         first = k_qkv[blk]
@@ -289,16 +281,10 @@
 
     QB = min(512, T * M)
     QH = QB // 2
-    if n == 128:
-        last = jnp.logical_and(t // 4 == 2 + c, lax.rem(t, 4) > 0)
-        first_blk = jnp.logical_and(t // 4 == 1 - c, lax.rem(t, 4) > 0)
-        owns = (jnp.logical_or(first_blk, last), last)
-        own_blk = t // 8
-        own_head = jnp.maximum(lax.rem(t, 4) - 1, 0)
-    else:
-        owns = (t < 2 * heads_w, t < heads_w)
-        own_blk = t // heads_w
-        own_head = lax.rem(t, heads_w)
+    place = t - spread * c
+    owns = (jnp.logical_and(place >= 0, place < 2 * heads_w), jnp.logical_and(place >= 0, place < heads_w))
+    own_blk = place // heads_w
+    own_head = lax.rem(place, heads_w)
 
     def attention(stage):
         land = G_O + own_blk if stage == 0 else G_OT
@@ -325,7 +311,7 @@
                 for q in range(QB // M):
                     tt = i * (QB // M) + q
                     mine = pl.ds(pl.multiple_of(tt * M, M), M)
-                    dst = gathered.at[land, :, head_cols(w, own_head)]
+                    dst = gathered.at[land, :, pl.ds(pl.multiple_of(w * C + own_head * HD, HD), HD)]
 
                     @pl.when(tt != t)
                     def _():
@@ -350,19 +336,17 @@
             lax.fori_loop(0, T, left, 0)
 
     def attention_gather(blk):
-        for h, ph in enumerate(att_phases(blk)):
+        for h in range(heads_w):
             @pl.when(owner(blk, h) != t)
             def _():
-                got = piece(ph, j, c)
+                got = gathered.at[G_ATT[blk], :, pl.ds(pl.multiple_of(w * C + h * HD, HD), HD)]
                 rcopy(got, got, o_send.at[0, t], o_recv.at[blk, h], partner).wait_recv()
-            gather_start(ph)
+        gather_start(PH_ATT[blk])
 
     def proj_block(blk):
         residual = (xh.at[PH_X], gathered.at[G_C0], gathered.at[G_A1])[blk]
-        for ph in att_phases(blk):
-            gather_forward(ph)
-        for ph in att_phases(blk):
-            gather_finish(ph)
+        gather_forward(PH_ATT[blk])
+        gather_finish(PH_ATT[blk])
         shared_matmul(gathered.at[G_ATT[blk]], k_proj[blk], residual, G_MID[blk], SH_U + blk)
 
     def up_block(blk):
@@ -414,33 +398,25 @@
             rcopy(sum_out.at[blk, s], sum_in.at[blk, s], sum_send.at[blk, s], sum_recv.at[blk, s], partner).wait_send()
 
     def down_rows():
-        def half_dot(m, core):
-            part = pl.ds(pl.multiple_of(core * FS, HD), FS)
-            return jnp.dot(hid[2, :, part], wbuf[(k_down[2] + m) % SLOTS, part, :], preferred_element_type=F32)
-
-        for m in range(4):
-            span = slice(m * C, (m + 1) * C)
-            if m < 2:
-                ready((k_down[2] + m) % SLOTS)
-                row_out[:, span] = half_dot(m, c)
         hidden_ready(2)
-        for m in range(4):
-            span = slice(m * C, (m + 1) * C)
-            row_out[:, span] = row_out[:, span] + half_dot(m, 1 - c) if m < 2 else matmul(hid[2], k_down[2] + m)
+        for half in range(2):
+            for m in (2 * half, 2 * half + 1):
+                row_out[:, m * C:(m + 1) * C] = matmul(hid[2], k_down[2] + m)
+            span = pl.ds(half * 2 * C, 2 * C)
             for r in FAR_FIRST:
                 for cc in ((c, 1 - c) if r else (1 - c,)):
                     to = near(r) * 2 + cc
                     out = row_out.at[pl.ds(pl.multiple_of(to * R, R), R), span]
-                    rcopy(out, row_in.at[w, :, span], row_send.at[m, to], row_recv.at[m, w], dev(t, near(r), cc)).start()
-        refill(k_down[2], 4)
+                    rcopy(out, row_in.at[w, :, span], row_send.at[half, to], row_recv.at[half, w], dev(t, near(r), cc)).start()
 
     def rows_finish():
         def arrive(ww, carry):
             @pl.when(ww != w)
             def _():
-                for m in range(4):
-                    got = row_in.at[ww, :, m * C:(m + 1) * C]
-                    rcopy(got, got, row_send.at[m, ww], row_recv.at[m, ww], partner).wait()
+                for half in range(2):
+                    span = pl.ds(half * 2 * C, 2 * C)
+                    got = row_in.at[ww, :, span]
+                    rcopy(got, got, row_send.at[half, ww], row_recv.at[half, ww], partner).wait()
             return carry
 
         lax.fori_loop(0, W, arrive, 0)
@@ -482,8 +458,8 @@
     proj_block(0)
     proj_block(1)
     up_block(1)
+    down_block(1)
     up_block(0)
-    down_block(1)
     down_block(0)
     gathered[G_C1, :, cols(w)] = down_finish(1)
     gather_start(PH_C1)
@@ -491,8 +467,7 @@
     gathered[G_U2, :, cols(w)] = down_finish(0)
     gather_start(PH_U2)
     gather_finish(PH_C1)
-    shared_dots(gathered.at[G_C1], k_zout, G_A1, 0, 4)
-    shared_add(gathered.at[G_U2], G_A1, SH_A1, PH_U2)
+    shared_matmul(gathered.at[G_C1], k_zout, gathered.at[G_U2], G_A1, SH_A1, PH_U2)
     shared_finish(G_A1, SH_A1)
     layer_norm(lambda row: gathered[G_A1, row, :])
     qkv_block(2, 1)
@@ -512,7 +487,7 @@
 
     lax.fori_loop(0, W, final_step, 0)
 
-    for ph in range(num_ph):
+    for ph in range(NUM_PH):
         gather_drain(ph)
     for sh in range(NUM_SH):
         shared_drain(sh)
@@ -560,13 +535,13 @@
                 pltpu.VMEM((2, M, C), F32),
                 pltpu.VMEM((M, D // 2), F32),
                 pltpu.VMEM((W, R, D // 2), F32),
-                dma((PH_O + 3 * heads_w, 7)), dma((PH_O + 3 * heads_w, 7)),
+                dma((NUM_PH, 7)), dma((NUM_PH, 7)),
                 dma((NUM_SH, 4)), dma((NUM_SH, 4)),
                 dma((3, 3, heads_w)), dma((2, T)),
                 dma((2, T)), dma((3, heads_w)),
                 dma((3, FS // C)), dma((3, FS // C)),
                 dma((2, 3)), dma((2, 3)),
-                dma((4, W)), dma((4, W)),
+                dma((2, W)), dma((2, W)),
             ],
             compiler_params=pltpu.CompilerParams(collective_id=0, has_side_effects=True, vmem_limit_bytes=67043328),
         )(

time: 113 us -> 113 us (level)
  no operation moved by 1% of the time
where the time goes in v3:
time: 113 us; the launch traced here: 112 us
  Pallas kernels  111 us (98%)
  local copies, waits for them, and re-layouts  1.42 us (1%)
    pallas_call x1, Pallas kernels, device_step(): pl.pallas_call(functools.partial(kernel, n, heads_w), out_shape=jax.Shape...  111 us

profile of v3, /device:TPU:1, one launch (start us, length us, event | category | flops | bytes accessed | tf_op | source)
XLA Modules:
  0.0 112.4 jit_solution(16130928245418734686)
XLA Ops:
  0.0 110.9 %shard_map.127 = bf16[8,3072]{1,0:T(8,128)(2,1)} custom-call(bf16[8,3072]{1,0:T(8,128)(2,1)} %bitcast.11, bf16[8,3072]{1,0:T(8,128)(2,1)} %bitcast.12, bf16[2,3072,9216]{2,1,0:T(8,128)(2,1)} %bitcast.2.in_qkv, bf16[2,3072,3072]{2,1,0:T(8,128)(2,1)} %bitcast.8, bf16[2,3072,12288]{2,1,0:T(8,128)(2,1)} %bitcast.4.in_up, ...), custom_call_target="tpu_custom_call" | custom-call | tf_op jit(solution)/shard_map/pallas_call | solution.py:516
  110.9 1.4 %copy.15 = bf16[1,8,3072]{2,1,0:T(8,128)(2,1)} copy(bf16[1,8,3072]{2,1,0:T(8,128)(2,1)} %bitcast.10) | data formatting | bytes 98304
